TPU v7x, 32 devices: a whole 2x2x4 slice. The times are simulated.
32 devices in a mesh: grp: 16 (over z, x, core), tp: 2 (over y).
Axes of the slice: x: 2, y: 2, z: 4, core: 2. Of those that a mesh axis runs over, the one named last changes fastest.
Arguments:
- memory_rows: bfloat16 [16384, 4096], P('grp', 'tp'), may hold values from -24 to 24, as said below
- norm_gain: float32 [4096], replicated, may hold values from 0.25 to 1.75
- key_weight: bfloat16 [4096, 4096], P(None, 'tp'), may hold values from -0.09375 to 0.09375
- owner_table: int32 [2048], replicated, may hold values from 0 to 2047, as said below
Outputs:
- placed_keys: bfloat16 [16384, 4096], P('grp', 'tp')
Inputs may be any that keep to these rules, and one draw needn't show every extreme that they name: A permutation of the 2048 block numbers. Block b of the input goes to block position owner_table[b], which lies in group owner_table[b] // 128. The 128 blocks of one group go to all 16 groups, exactly 8 blocks to each of them. `memory_rows`: rows have offsets and scales of their own, and features a common pattern.
All inputs are finite; a program needn't handle non-finite values.
Results may differ from a plain program's by a relative error of at most 0.0049.
Values may be sent and summed in bfloat16 or wider, within the bound.
A program may use at most 64 MiB of HBM per device.

v0:
```python
import functools

import jax
import jax.numpy as jnp
from jax import lax
from jax.experimental import pallas as pl
from jax.experimental.pallas import tpu as pltpu
from jax.sharding import PartitionSpec as P

BLK_ROWS = 8
EPS = 1e-05
CHUNKS = 16
MIB = 1024 * 1024
MESH = pl.DeviceIdType.MESH


def flipped(me, mask, groups):
    out = me
    bit = 1
    while bit < groups:
        out = out + ((mask // bit) % 2) * bit * (1 - 2 * ((me // bit) % 2))
        bit *= 2
    return out


def mask_at(me, step, groups):
    quarter = groups // 4
    inner = ((me // quarter + 1) // 2) % 2
    turn = step // quarter
    first = (3 - turn) // 3
    second = (turn % 2) * (1 - turn // 2)
    third = (turn // 2) * (1 - turn % 2)
    far = first * (1 + inner) + 3 * second + third * (2 - inner)
    return far * quarter + quarter - 1 - step % quarter


def peer_mask(me, step, groups, early):
    regular = groups - early
    split = groups // 2 - early
    is_early = step // regular
    after = (1 + step // split) // 2
    late = step - regular + split
    return mask_at(me, is_early * late + (1 - is_early) * (step + early * after), groups)


def index_kernel(groups, per_chunk, table_ref, slot_ref, index_ref):
    me = lax.axis_index("grp")
    blocks = table_ref.shape[1]
    capacity = blocks // groups

    lane = lax.broadcasted_iota(jnp.int32, (groups, blocks), 1)
    row = lax.broadcasted_iota(jnp.int32, (groups, blocks), 0)
    peer = jnp.zeros((groups, blocks), jnp.int32)
    for step in range(groups):
        mask = peer_mask(me, step, groups, per_chunk)
        peer = jnp.where(row == step, flipped(me, mask, groups), peer)

    def ranked(offset, value):
        chosen = (offset >= 0) & (offset < blocks)
        counted = chosen.astype(jnp.int32)
        shift = 1
        while shift < blocks:
            counted = counted + jnp.where(lane >= shift, pltpu.roll(counted, shift, 1), 0)
            shift *= 2
        result = jnp.zeros((groups, blocks), jnp.int32)
        for r in range(capacity):
            at_rank = jnp.where(chosen & (counted == r + 1), value, 0).astype(jnp.float32)
            found = jnp.sum(at_rank, axis=1, keepdims=True).astype(jnp.int32)
            result = jnp.where(lane == r, found, result)
        return result

    own = jnp.broadcast_to(table_ref[pl.ds(me, 1), :], (groups, blocks))
    index_ref[...] = ranked(own - peer * blocks, lane)
    offset = table_ref[...] - me * blocks
    slot_ref[...] = ranked(offset, offset)


def place_kernel(groups, slot_ref, in_ref, out_ref, sem):
    me = lax.axis_index("grp")
    blocks = in_ref.shape[0]
    capacity = blocks // groups

    def move(i, carry):
        mask = i // capacity
        slot = slot_ref[me ^ mask, i - mask * capacity]
        pltpu.make_async_copy(in_ref.at[i], out_ref.at[slot], sem).start()
        return carry

    lax.fori_loop(0, blocks, move, 0, unroll=8)
    pltpu.make_async_copy(in_ref, out_ref, sem).wait()


def main_kernel(
    groups, parts, index_ref, rows_ref, gain_ref, weight_ref, out_ref,
    raw, away, mine, others, weight, keys, normed, gains,
    raw_sem, early_send, early_recv, weight_sem, gain_sem, gather_send, gather_recv, key_send, key_recv, self_sem,
):
    me = lax.axis_index("grp")
    part = lax.axis_index("tp")
    blocks, _, depth = rows_ref.shape
    row_count = blocks * BLK_ROWS
    width = depth * parts
    chunk = row_count // CHUNKS
    chunk_blocks = blocks // CHUNKS
    capacity = blocks // groups
    per_chunk = groups // CHUNKS
    piece = row_count // groups
    regular = groups - per_chunk

    barrier = pltpu.get_barrier_semaphore()
    def greet(i, carry):
        mask = groups - i
        pl.semaphore_signal(
            barrier, inc=1, device_id={"grp": flipped(me, mask, groups)}, device_id_type=MESH
        )
        return carry

    lax.fori_loop(1, groups, greet, 0)
    for j in range(1, parts):
        pl.semaphore_signal(
            barrier, inc=1, device_id={"tp": (part + j) % parts}, device_id_type=MESH
        )

    raw_copy = pltpu.make_async_copy(rows_ref, raw, raw_sem)

    def weight_copy(j):
        origin = (part + j) % parts
        return pltpu.make_async_copy(
            weight_ref.at[pl.ds(pl.multiple_of(origin * depth, depth), depth)],
            weight.at[pl.ds(j * depth, depth)],
            weight_sem.at[j],
        )

    def gain_copy(j):
        origin = (part + j) % parts
        return pltpu.make_async_copy(
            gain_ref.at[:, pl.ds(pl.multiple_of(origin * depth, depth), depth)],
            gains.at[:, pl.ds(j * depth, depth)],
            gain_sem.at[j],
        )

    def gather_copy(c, j):
        at = pl.ds(c * chunk_blocks, chunk_blocks)
        return pltpu.make_async_remote_copy(
            src_ref=mine.at[at],
            dst_ref=others.at[j - 1, at],
            send_sem=gather_send.at[j - 1, c],
            recv_sem=gather_recv.at[j - 1, c],
            device_id={"tp": (part + parts - j) % parts},
            device_id_type=MESH,
        )

    def key_copy(step):
        mask = peer_mask(me, step, groups, per_chunk)
        return pltpu.make_async_remote_copy(
            src_ref=keys.at[pl.ds(step * piece, piece)],
            dst_ref=out_ref.at[pl.ds(mask * piece, piece)],
            send_sem=key_send.at[step],
            recv_sem=key_recv.at[mask],
            device_id={"grp": flipped(me, mask, groups)},
            device_id_type=MESH,
        )

    def local_copy(i):
        step = regular + i if i < per_chunk else regular - 1
        mask = peer_mask(me, step, groups, per_chunk)
        return pltpu.make_async_copy(
            keys.at[pl.ds(step * piece, piece)],
            out_ref.at[pl.ds(mask * piece, piece)],
            self_sem.at[i],
        )

    def early_copy(i):
        mask = peer_mask(me, regular + i, groups, per_chunk)
        return pltpu.make_async_remote_copy(
            src_ref=away.at[pl.ds(i * capacity, capacity)],
            dst_ref=mine.at[pl.ds((regular + i) * capacity, capacity)],
            send_sem=early_send.at[i],
            recv_sem=early_recv.at[i],
            device_id={"grp": flipped(me, mask, groups)},
            device_id_type=MESH,
        )

    raw_copy.start()

    for j in range(parts):
        gain_copy(j).start()
    raw_copy.wait()
    for j in range(parts):
        weight_copy(j).start()

    def arrange(c):
        def take(i, carry):
            step = i // capacity
            block = raw[index_ref[step, i - step * capacity]]
            if c == CHUNKS - 1:
                away[i - c * chunk_blocks] = block
            else:
                mine[i] = block
            return carry

        lax.fori_loop(c * chunk_blocks, (c + 1) * chunk_blocks, take, 0, unroll=2)

    arrange(0)
    pl.semaphore_wait(barrier, groups - 1 + parts - 1)
    for c in range(CHUNKS - 1):
        if c > 0:
            arrange(c)
        for j in range(1, parts):
            gather_copy(c, j).start()
        if c == 0:
            arrange(CHUNKS - 1)
            for i in range(per_chunk):
                early_copy(i).start()
    for j in range(parts):
        gain_copy(j).wait()
        weight_copy(j).wait()

    sub = 2 * BLK_ROWS
    tile = depth

    def one_chunk(c, carry):
        base = pl.multiple_of(c * chunk, chunk)

        @pl.when(c == CHUNKS // 2)
        def _():
            for i in range(per_chunk):
                early_copy(i).wait_recv()
            for j in range(1, parts):
                gather_copy(CHUNKS - 1, j).start()

        for j in range(1, parts):
            gather_copy(c, j).wait_recv()

        def norm_rows(i, carry):
            at = pl.ds(c * chunk_blocks + i * 2, 2)
            to = pl.ds(pl.multiple_of(i * sub, sub), sub)

            def values(j):
                held = mine[at] if j == 0 else others[j - 1, at]
                return held.astype(jnp.float32).reshape(sub, depth)

            row_sum = 0.0
            row_sq = 0.0
            for j in range(parts):
                x = values(j)
                row_sum = row_sum + jnp.sum(x, axis=1, keepdims=True)
                row_sq = row_sq + jnp.sum(x * x, axis=1, keepdims=True)
            mean = row_sum / width
            scale = lax.rsqrt(row_sq / width - mean * mean + EPS)
            for j in range(parts):
                cols = pl.ds(j * depth, depth)
                normed[to, cols] = ((values(j) - mean) * scale * gains[:, cols]).astype(
                    jnp.bfloat16
                )
            return carry

        lax.fori_loop(0, chunk // sub, norm_rows, 0)

        def columns(n, carry):
            cols = pl.ds(pl.multiple_of(n * tile, tile), tile)
            keys[pl.ds(base, chunk), cols] = jnp.dot(
                normed[...], weight[:, cols], preferred_element_type=jnp.float32
            ).astype(jnp.bfloat16)
            return carry

        lax.fori_loop(0, keys.shape[1] // tile, columns, 0)

        for i in range(per_chunk):
            step = c * per_chunk + i

            @pl.when(step < regular - 1)
            def _():
                key_copy(step).start()

        @pl.when(c == CHUNKS - 2)
        def _():
            local_copy(per_chunk).start()

        return carry

    lax.fori_loop(0, CHUNKS, one_chunk, 0)

    for i in range(per_chunk):
        local_copy(i).start()
    for i in range(per_chunk):
        early_copy(i).wait_send()
    for c in range(CHUNKS):
        for j in range(1, parts):
            gather_copy(c, j).wait_send()

    def finish(step, carry):
        key_copy(step).wait()
        return carry

    lax.fori_loop(0, regular - 1, finish, 0)
    for i in range(per_chunk + 1):
        local_copy(i).wait()


def on_device(groups, parts, memory_rows, norm_gain, key_weight, owner_table):
    row_count, depth = memory_rows.shape
    columns = key_weight.shape[1]
    blocks = row_count // BLK_ROWS
    capacity = blocks // groups
    any_space = pl.BlockSpec(memory_space=pl.ANY)
    in_hbm = pl.BlockSpec(memory_space=pltpu.HBM)
    in_vmem = pl.BlockSpec(memory_space=pltpu.VMEM)
    in_smem = pl.BlockSpec(memory_space=pltpu.SMEM)

    dma = pltpu.SemaphoreType.DMA
    listing = jax.ShapeDtypeStruct((groups, blocks), jnp.int32)
    slots, index = pl.pallas_call(
        functools.partial(index_kernel, groups, groups // CHUNKS),
        out_shape=[listing, listing],
        in_specs=[in_vmem],
        out_specs=[in_vmem, in_vmem],
        compiler_params=pltpu.CompilerParams(vmem_limit_bytes=4 * MIB),
        name="index",
    )(owner_table.reshape(groups, blocks))

    incoming = pl.pallas_call(
        functools.partial(main_kernel, groups, parts),
        out_shape=jax.ShapeDtypeStruct((row_count, columns), jnp.bfloat16),
        in_specs=[in_smem, in_hbm, in_hbm, in_hbm],
        out_specs=any_space,
        scratch_shapes=[
            pltpu.VMEM((blocks, BLK_ROWS, depth), jnp.bfloat16),
            pltpu.VMEM((blocks // CHUNKS, BLK_ROWS, depth), jnp.bfloat16),
            pltpu.VMEM((blocks, BLK_ROWS, depth), jnp.bfloat16),
            pltpu.VMEM((parts - 1, blocks, BLK_ROWS, depth), jnp.bfloat16),
            pltpu.VMEM((depth * parts, columns), jnp.bfloat16),
            pltpu.VMEM((row_count, columns), jnp.bfloat16),
            pltpu.VMEM((row_count // CHUNKS, depth * parts), jnp.bfloat16),
            pltpu.VMEM((1, depth * parts), jnp.float32),
            dma,
            dma((groups // CHUNKS,)),
            dma((groups // CHUNKS,)),
            dma((parts,)),
            dma((parts,)),
            dma((parts - 1, CHUNKS)),
            dma((parts - 1, CHUNKS)),
            dma((groups,)),
            dma((groups,)),
            dma((groups // CHUNKS + 1,)),
        ],
        compiler_params=pltpu.CompilerParams(
            collective_id=0, has_side_effects=True, vmem_limit_bytes=48 * MIB
        ),
        name="exchange",
    )(index, memory_rows.reshape(blocks, BLK_ROWS, depth), norm_gain[None, :], key_weight)

    placed = pl.pallas_call(
        functools.partial(place_kernel, groups),
        out_shape=jax.ShapeDtypeStruct((blocks, BLK_ROWS, columns), jnp.bfloat16),
        in_specs=[in_smem, in_vmem],
        out_specs=any_space,
        scratch_shapes=[pltpu.SemaphoreType.DMA],
        compiler_params=pltpu.CompilerParams(vmem_limit_bytes=16 * MIB),
        name="place",
    )(slots, incoming.reshape(blocks, BLK_ROWS, columns))
    return placed.reshape(row_count, columns)


def solution(mesh):
    in_specs = (P("grp", "tp"), P(), P(None, "tp"), P())
    out_specs = P("grp", "tp")
    return jax.shard_map(
        functools.partial(on_device, mesh.shape["grp"], mesh.shape["tp"]),
        mesh=mesh, in_specs=in_specs, out_specs=out_specs, check_vma=False,
    )
```

profile of v0, /device:TPU:0, one launch (start us, length us, event | category | flops | bytes accessed | tf_op | source)
XLA Modules:
  0.0 108.8 jit_solution(6932618381239002100)
XLA Ops:
  0.0 0.0 copy-start.1
  0.0 0.7 copy-done.1
  0.7 0.7 index.1
  1.4 0.0 copy-start
  1.4 0.7 copy-done
  2.1 104.1 %exchange.1 = bf16[1024,2048]{1,0:T(8,128)(2,1)S(1)} custom-call(s32[16,128]{1,0:T(8,128)S(1)} %get-tuple-element.8.index_ref, bf16[128,8,2048]{2,1,0:T(8,128)(2,1)} %bitcast.8, f32[1,4096]{1,0:T(1,128)S(1)} %bitcast.6, bf16[4096,2048]{1,0:T(8,128)(2,1)} %weight_ref.1), custom_call_target="tpu_custom_call" | custom-call | tf_op jit(solution)/shard_map/exchange/pallas_call | solution.py:322
  106.2 2.6 %place.1 = bf16[128,8,2048]{2,1,0:T(8,128)(2,1)} custom-call(s32[16,128]{1,0:T(8,128)S(1)} %get-tuple-element.7.slot_ref, bf16[128,8,2048]{2,1,0:T(8,128)(2,1)S(1)} %bitcast.5), custom_call_target="tpu_custom_call" | custom-call | tf_op jit(solution)/shard_map/place/pallas_call | solution.py:353
Async XLA Ops:
  0.0 0.7 copy-start.1
  1.4 0.7 copy-start
where the time goes:
time: 109 us
  Pallas kernels  107 us (98%)
  local copies, waits for them, and re-layouts  1.41 us (1%)
    pallas_call x1, Pallas kernels, on_device(): pl.pallas_call(functools.partial(main_kernel, groups, parts), out_shape=j...  104 us
    pallas_call x1, Pallas kernels, on_device(): pl.pallas_call(functools.partial(place_kernel, groups), out_shape=jax.Sha...  2.65 us

commit v1 on v0

v1 whole, which is shorter than its diff:
```python
import functools

import jax
import jax.numpy as jnp
from jax import lax
from jax.experimental import pallas as pl
from jax.experimental.pallas import tpu as pltpu
from jax.sharding import PartitionSpec as P

BLK_ROWS = 8
EPS = 1e-05
CHUNKS = 16
LEAD = 4
TAIL = 2
STATS_AT = 4
HALF_AT = 9
SLICE = 256
LANES = 128
LOADS = 8
MIB = 1024 * 1024
MESH = pl.DeviceIdType.MESH


def flipped(me, mask, groups):
    out = me
    bit = 1
    while bit < groups:
        out = out + ((mask // bit) % 2) * bit * (1 - 2 * ((me // bit) % 2))
        bit *= 2
    return out


def mask_at(me, step, groups):
    quarter = groups // 4
    inner = ((me // quarter + 1) // 2) % 2
    turn = step // quarter
    first = (3 - turn) // 3
    second = (turn % 2) * (1 - turn // 2)
    third = (turn // 2) * (1 - turn % 2)
    far = first * (1 + inner) + 3 * second + third * (2 - inner)
    return far * quarter + quarter - 1 - step % quarter


def peer_mask(me, step, groups, early):
    regular = groups - early
    split = groups // 2 - early
    is_early = step // regular
    after = (1 + step // split) // 2
    late = step - regular + split
    return mask_at(me, is_early * late + (1 - is_early) * (step + early * after), groups)


def ranked(offset, value, capacity):
    groups, blocks = offset.shape
    lane = lax.broadcasted_iota(jnp.int32, (groups, blocks), 1)
    chosen = (offset >= 0) & (offset < blocks)
    counted = chosen.astype(jnp.int32)
    shift = 1
    while shift < blocks:
        counted = counted + jnp.where(lane >= shift, pltpu.roll(counted, shift, 1), 0)
        shift *= 2
    result = jnp.zeros((groups, blocks), jnp.int32)
    for r in range(capacity):
        at_rank = jnp.where(chosen & (counted == r + 1), value, 0).astype(jnp.float32)
        found = jnp.sum(at_rank, axis=1, keepdims=True).astype(jnp.int32)
        result = jnp.where(lane == r, found, result)
    return result


def place_kernel(groups, slot_ref, in_ref, out_ref, sem):
    me = lax.axis_index("grp")
    blocks = in_ref.shape[0]
    capacity = blocks // groups

    def move(mask, carry):
        for r in range(capacity):
            slot = slot_ref[me ^ mask, r]
            pltpu.make_async_copy(in_ref.at[mask * capacity + r], out_ref.at[slot], sem).start()
        return carry

    lax.fori_loop(0, groups, move, 0)
    pltpu.make_async_copy(in_ref, out_ref, sem).wait()


def main_kernel(
    groups, parts, table_ref, rows_ref, gain_ref, weight_ref, out_ref, slot_ref,
    table, listed, index, raw, away, mine, others, weight, keys, normed, ready, gains, total,
    columns_stat, own_stat, peer_stat, means, scales,
    table_sem, index_sem, raw_sem, early_send, early_recv, weight_sem, gain_sem, gather_send, gather_recv,
    last_send, last_recv, stat_send, stat_recv, key_send, key_recv,
):
    me = lax.axis_index("grp")
    part = lax.axis_index("tp")
    blocks, _, depth = rows_ref.shape
    row_count = blocks * BLK_ROWS
    width = depth * parts
    chunk = row_count // CHUNKS
    chunk_blocks = blocks // CHUNKS
    capacity = blocks // groups
    per_chunk = groups // CHUNKS
    piece = row_count // groups
    regular = groups - per_chunk
    last = CHUNKS - 1
    body = CHUNKS - TAIL
    tail = TAIL * chunk
    tail_blocks = TAIL * chunk_blocks
    slice_width = min(SLICE, depth)
    slices = depth // slice_width
    sub = 2 * BLK_ROWS

    table_copy = pltpu.make_async_copy(table_ref, table, table_sem)
    table_copy.start()
    loads = min(LOADS, blocks)
    for i in range(loads):
        at = pl.ds(i * (blocks // loads), blocks // loads)
        pltpu.make_async_copy(rows_ref.at[at], raw.at[at], raw_sem).start()
    gain_copy = pltpu.make_async_copy(gain_ref, gains, gain_sem)
    gain_copy.start()

    barrier = pltpu.get_barrier_semaphore()

    def greet(i, carry):
        mask = groups - i
        pl.semaphore_signal(
            barrier, inc=1, device_id={"grp": flipped(me, mask, groups)}, device_id_type=MESH
        )
        return carry

    lax.fori_loop(1, groups, greet, 0)
    for j in range(1, parts):
        pl.semaphore_signal(
            barrier, inc=1, device_id={"tp": (part + j) % parts}, device_id_type=MESH
        )

    def weight_copy(j):
        origin = (part + j) % parts
        return pltpu.make_async_copy(
            weight_ref.at[pl.ds(pl.multiple_of(origin * depth, depth), depth)],
            weight.at[pl.ds(j * depth, depth)],
            weight_sem.at[j],
        )

    def gain_at(j, first, count):
        origin = (part + j) % parts
        return gains[:, pl.ds(pl.multiple_of(origin * depth + first, LANES), count)]

    def gather_copy(c, j):
        at = pl.ds(c * chunk_blocks, chunk_blocks)
        return pltpu.make_async_remote_copy(
            src_ref=mine.at[at],
            dst_ref=others.at[j - 1, at],
            send_sem=gather_send.at[j - 1, c],
            recv_sem=gather_recv.at[j - 1, c],
            device_id={"tp": (part + parts - j) % parts},
            device_id_type=MESH,
        )

    def last_copy(j, s):
        at = pl.ds(body * chunk_blocks, tail_blocks)
        cols = pl.ds(pl.multiple_of(s * slice_width, slice_width), slice_width)
        return pltpu.make_async_remote_copy(
            src_ref=mine.at[at, :, cols],
            dst_ref=others.at[j - 1, at, :, cols],
            send_sem=last_send.at[j - 1, s],
            recv_sem=last_recv.at[j - 1, s],
            device_id={"tp": (part + parts - j) % parts},
            device_id_type=MESH,
        )

    def stat_copy(j):
        return pltpu.make_async_remote_copy(
            src_ref=own_stat,
            dst_ref=peer_stat.at[j - 1],
            send_sem=stat_send.at[j - 1],
            recv_sem=stat_recv.at[j - 1],
            device_id={"tp": (part + parts - j) % parts},
            device_id_type=MESH,
        )

    def key_copy(step):
        mask = peer_mask(me, step, groups, per_chunk)
        return pltpu.make_async_remote_copy(
            src_ref=keys.at[pl.ds(step * piece, piece)],
            dst_ref=out_ref.at[pl.ds(mask * piece, piece)],
            send_sem=key_send.at[step],
            recv_sem=key_recv.at[mask],
            device_id={"grp": flipped(me, mask, groups)},
            device_id_type=MESH,
        )

    def early_copy(i):
        mask = peer_mask(me, regular + i, groups, per_chunk)
        return pltpu.make_async_remote_copy(
            src_ref=away.at[pl.ds(i * capacity, capacity)],
            dst_ref=mine.at[pl.ds((regular + i) * capacity, capacity)],
            send_sem=early_send.at[i],
            recv_sem=early_recv.at[i],
            device_id={"grp": flipped(me, mask, groups)},
            device_id_type=MESH,
        )

    def arrange(c):
        def take(i, carry):
            step = i // capacity
            at = index[step, i - step * capacity]
            block = raw[jnp.minimum(jnp.maximum(at, 0), blocks - 1)]
            if c == last:
                away[i - c * chunk_blocks] = block
            else:
                mine[i] = block
            return carry

        lax.fori_loop(c * chunk_blocks, (c + 1) * chunk_blocks, take, 0, unroll=2)

    row = lax.broadcasted_iota(jnp.int32, (groups, blocks), 0)
    lane = lax.broadcasted_iota(jnp.int32, (groups, blocks), 1)
    peer = jnp.zeros((groups, blocks), jnp.int32)
    for step in range(groups):
        mask = peer_mask(me, step, groups, per_chunk)
        peer = jnp.where(row == step, flipped(me, mask, groups), peer)
    table_copy.wait()
    own = jnp.broadcast_to(table[pl.ds(me, 1), :], (groups, blocks))
    listed[...] = ranked(own - peer * blocks, lane, capacity)
    index_copy = pltpu.make_async_copy(listed, index, index_sem)
    index_copy.start()
    index_copy.wait()
    pltpu.make_async_copy(rows_ref, raw, raw_sem).wait()
    for j in range(parts):
        weight_copy(j).start()

    arrange(0)
    arrange(last)
    pl.semaphore_wait(barrier, groups - 1 + parts - 1)
    for j in range(1, parts):
        gather_copy(0, j).start()
    for i in range(per_chunk):
        early_copy(i).start()
    for c in range(1, last):
        arrange(c)
        if c < LEAD:
            for j in range(1, parts):
                gather_copy(c, j).start()

    offset = table[...] - me * blocks
    slot_ref[...] = ranked(offset, offset, capacity)
    columns_stat[...] = jnp.zeros_like(columns_stat)
    gain_copy.wait()
    for j in range(parts):
        weight_copy(j).wait()

    def stored(c, i, j, first, count):
        at = pl.ds(c * chunk_blocks + i * 2, 2)
        cols = pl.ds(first, count)
        held = mine[at, :, cols] if j == 0 else others[j - 1, at, :, cols]
        return held.astype(jnp.float32).reshape(sub, count)

    def rows_at(i):
        return pl.ds(pl.multiple_of(i * sub, sub), sub)

    def own_sums():
        def sums(i, carry):
            x = stored(body, i, 0, 0, depth)
            row_sum = jnp.sum(x, axis=1, keepdims=True)
            row_sq = jnp.sum(x * x, axis=1, keepdims=True)
            where = lax.broadcasted_iota(jnp.int32, (sub, LANES), 1)
            columns_stat[rows_at(i), :] = jnp.where(
                where == 0, row_sum, jnp.where(where == 1, row_sq, 0.0)
            )
            return carry

        lax.fori_loop(0, tail // sub, sums, 0)
        own_stat[...] = jnp.transpose(columns_stat[...])[:BLK_ROWS]

    def all_sums():
        sums = own_stat[...]
        for j in range(1, parts):
            sums = sums + peer_stat[j - 1]
        columns_stat[:BLK_ROWS, :] = sums
        columns = jnp.transpose(columns_stat[...])[:tail]
        mean = columns[:, 0:1] / width
        means[...] = jnp.broadcast_to(mean, means.shape)
        scale = lax.rsqrt(columns[:, 1:2] / width - mean * mean + EPS)
        scales[...] = jnp.broadcast_to(scale, scales.shape)

    def last_norm(j, first, count):
        def norm_rows(i, carry):
            for k in range(count // LANES):
                at = pl.multiple_of(first + k * LANES, LANES)
                x = stored(body, i, j, at, LANES)
                ready[rows_at(i), pl.ds(pl.multiple_of(j * depth + at, LANES), LANES)] = (
                    (x - means[rows_at(i), :]) * scales[rows_at(i), :] * gain_at(j, at, LANES)
                ).astype(jnp.bfloat16)
            return carry

        lax.fori_loop(0, tail // sub, norm_rows, 0, unroll=count <= SLICE)

    def last_product(j, first, count):
        at = pl.ds(pl.multiple_of(j * depth + first, LANES), count)
        return jnp.dot(ready[:, at], weight[at, :], preferred_element_type=jnp.float32)

    def one_chunk(c, carry):
        base = pl.multiple_of(c * chunk, chunk)

        @pl.when(c == STATS_AT)
        def _():
            for i in range(per_chunk):
                early_copy(i).wait_recv()
            own_sums()
            for j in range(1, parts):
                stat_copy(j).start()

        @pl.when(c == HALF_AT)
        def _():
            for j in range(1, parts):
                stat_copy(j).wait_recv()
            all_sums()
            last_norm(0, 0, depth)
            total[...] = last_product(0, 0, depth)

        for j in range(1, parts):
            gather_copy(c, j).wait_recv()

        @pl.when(c + LEAD < body)
        def _():
            for j in range(1, parts):
                gather_copy(c + LEAD, j).start()

        @pl.when(c + LEAD == body)
        def _():
            def send(s, carry):
                for j in range(1, parts):
                    last_copy(j, s).start()
                return carry

            lax.fori_loop(0, slices, send, 0)

        def norm_rows(i, carry):
            row_sum = 0.0
            row_sq = 0.0
            for j in range(parts):
                x = stored(c, i, j, 0, depth)
                row_sum = row_sum + jnp.sum(x, axis=1, keepdims=True)
                row_sq = row_sq + jnp.sum(x * x, axis=1, keepdims=True)
            mean = row_sum / width
            scale = lax.rsqrt(row_sq / width - mean * mean + EPS)
            for j in range(parts):
                normed[rows_at(i), pl.ds(j * depth, depth)] = (
                    (stored(c, i, j, 0, depth) - mean) * scale * gain_at(j, 0, depth)
                ).astype(jnp.bfloat16)
            return carry

        lax.fori_loop(0, chunk // sub, norm_rows, 0)
        keys[pl.ds(base, chunk), :] = jnp.dot(
            normed[...], weight[...], preferred_element_type=jnp.float32
        ).astype(jnp.bfloat16)

        for i in range(per_chunk):
            key_copy(c * per_chunk + i).start()

        return carry

    lax.fori_loop(0, body, one_chunk, 0)

    def last_slice(s, j):
        first = s * slice_width
        last_copy(j, s).wait_recv()
        last_norm(j, first, slice_width)
        return last_product(j, first, slice_width)

    def add_slice(s, carry):
        for j in range(1, parts):
            total[...] += last_slice(s, j)
        return carry

    lax.fori_loop(0, slices - 1, add_slice, 0)
    for j in range(1, parts - 1):
        total[...] += last_slice(slices - 1, j)
    done = (total[...] + last_slice(slices - 1, parts - 1)).astype(jnp.bfloat16)
    for step in range(body * per_chunk, groups):
        rows = done[step * piece - body * chunk :][:piece]
        if step < regular - 1:
            keys[pl.ds(step * piece, piece), :] = rows
            key_copy(step).start()
        else:
            mask = peer_mask(me, step, groups, per_chunk)
            out_ref[pl.ds(pl.multiple_of(mask * piece, piece), piece), :] = rows

    for i in range(per_chunk):
        early_copy(i).wait_send()
    for j in range(1, parts):
        stat_copy(j).wait_send()

    def sent(c, carry):
        for j in range(1, parts):
            gather_copy(c, j).wait_send()
        return carry

    lax.fori_loop(0, body, sent, 0)

    def last_sent(s, carry):
        for j in range(1, parts):
            last_copy(j, s).wait_send()
        return carry

    lax.fori_loop(0, slices, last_sent, 0)

    def finish(step, carry):
        key_copy(step).wait()
        return carry

    lax.fori_loop(0, regular - 1, finish, 0)


def on_device(groups, parts, memory_rows, norm_gain, key_weight, owner_table):
    row_count, depth = memory_rows.shape
    columns = key_weight.shape[1]
    blocks = row_count // BLK_ROWS
    chunk = row_count // CHUNKS
    per_chunk = groups // CHUNKS
    slices = depth // min(SLICE, depth)
    any_space = pl.BlockSpec(memory_space=pl.ANY)
    in_hbm = pl.BlockSpec(memory_space=pltpu.HBM)
    in_vmem = pl.BlockSpec(memory_space=pltpu.VMEM)
    in_smem = pl.BlockSpec(memory_space=pltpu.SMEM)

    def kept(x):
        return pltpu.with_memory_space_constraint(x, pltpu.HBM)

    dma = pltpu.SemaphoreType.DMA
    incoming, slots = pl.pallas_call(
        functools.partial(main_kernel, groups, parts),
        out_shape=[
            jax.ShapeDtypeStruct((row_count, columns), jnp.bfloat16),
            jax.ShapeDtypeStruct((groups, blocks), jnp.int32),
        ],
        in_specs=[in_hbm, in_hbm, in_hbm, in_hbm],
        out_specs=[in_vmem, in_vmem],
        scratch_shapes=[
            pltpu.VMEM((groups, blocks), jnp.int32),
            pltpu.VMEM((groups, blocks), jnp.int32),
            pltpu.SMEM((groups, blocks), jnp.int32),
            pltpu.VMEM((blocks, BLK_ROWS, depth), jnp.bfloat16),
            pltpu.VMEM((blocks // CHUNKS, BLK_ROWS, depth), jnp.bfloat16),
            pltpu.VMEM((blocks, BLK_ROWS, depth), jnp.bfloat16),
            pltpu.VMEM((parts - 1, blocks, BLK_ROWS, depth), jnp.bfloat16),
            pltpu.VMEM((depth * parts, columns), jnp.bfloat16),
            pltpu.VMEM((row_count, columns), jnp.bfloat16),
            pltpu.VMEM((chunk, depth * parts), jnp.bfloat16),
            pltpu.VMEM((TAIL * chunk, depth * parts), jnp.bfloat16),
            pltpu.VMEM((1, depth * parts), jnp.float32),
            pltpu.VMEM((TAIL * chunk, columns), jnp.float32),
            pltpu.VMEM((LANES, LANES), jnp.float32),
            pltpu.VMEM((BLK_ROWS, LANES), jnp.float32),
            pltpu.VMEM((parts - 1, BLK_ROWS, LANES), jnp.float32),
            pltpu.VMEM((TAIL * chunk, LANES), jnp.float32),
            pltpu.VMEM((TAIL * chunk, LANES), jnp.float32),
            dma,
            dma,
            dma,
            dma((per_chunk,)),
            dma((per_chunk,)),
            dma((parts,)),
            dma,
            dma((parts - 1, CHUNKS)),
            dma((parts - 1, CHUNKS)),
            dma((parts - 1, slices)),
            dma((parts - 1, slices)),
            dma((parts - 1,)),
            dma((parts - 1,)),
            dma((groups,)),
            dma((groups,)),
        ],
        compiler_params=pltpu.CompilerParams(
            collective_id=0, has_side_effects=True, vmem_limit_bytes=48 * MIB
        ),
        name="exchange",
    )(
        kept(owner_table.reshape(groups, blocks)),
        kept(memory_rows.reshape(blocks, BLK_ROWS, depth)),
        kept(norm_gain[None, :]),
        kept(key_weight),
    )

    placed = pl.pallas_call(
        functools.partial(place_kernel, groups),
        out_shape=jax.ShapeDtypeStruct((blocks, BLK_ROWS, columns), jnp.bfloat16),
        in_specs=[in_smem, in_vmem],
        out_specs=any_space,
        scratch_shapes=[pltpu.SemaphoreType.DMA],
        compiler_params=pltpu.CompilerParams(vmem_limit_bytes=16 * MIB),
        name="place",
    )(slots, incoming.reshape(blocks, BLK_ROWS, columns))
    return placed.reshape(row_count, columns)


def solution(mesh):
    in_specs = (P("grp", "tp"), P(), P(None, "tp"), P())
    out_specs = P("grp", "tp")
    return jax.shard_map(
        functools.partial(on_device, mesh.shape["grp"], mesh.shape["tp"]),
        mesh=mesh, in_specs=in_specs, out_specs=out_specs, check_vma=False,
    )
```

time: 109 us -> 104 us (0.954)
  Pallas kernels: 107 us -> 103 us
  local copies, waits for them, and re-layouts: 1.41 us -> 0 us
    pallas_call x2 -> x1, Pallas kernels: 105 us -> 100 us  [on_device(): pl.pallas_call(functools.partial(main_kernel, groups, parts), out_shape=[...]
    unnamed x4 -> x0, local copies, waits for them, and re-layouts: 1.41 us -> none
where the time goes in v1:
time: 104 us; the launch traced here: 103 us
  Pallas kernels  103 us (99%)
    pallas_call x1, Pallas kernels, on_device(): pl.pallas_call(functools.partial(main_kernel, groups, parts), out_shape=[...  100 us
    pallas_call x1, Pallas kernels, on_device(): pl.pallas_call(functools.partial(place_kernel, groups), out_shape=jax.Sha...  2.64 us

profile of v1, /device:TPU:0, one launch (start us, length us, event | category | flops | bytes accessed | tf_op | source)
XLA Modules:
  0.0 103.1 jit_solution(11903944036736142734)
XLA Ops:
  0.0 100.4 %exchange.1 = (bf16[1024,2048]{1,0:T(8,128)(2,1)S(1)}, s32[16,128]{1,0:T(8,128)S(1)}) custom-call(s32[16,128]{1,0:T(8,128)} %bitcast.8, bf16[128,8,2048]{2,1,0:T(8,128)(2,1)} %bitcast.6, f32[1,4096]{1,0:T(1,128)} %bitcast.7, bf16[4096,2048]{1,0:T(8,128)(2,1)} %weight_ref.1), custom_call_target="tpu_custom_call" | custom-call | tf_op jit(solution)/shard_map/exchange/pallas_call | solution.py:430
  100.4 2.6 %place.1 = bf16[128,8,2048]{2,1,0:T(8,128)(2,1)} custom-call(s32[16,128]{1,0:T(8,128)S(1)} %get-tuple-element.7.slot_ref, bf16[128,8,2048]{2,1,0:T(8,128)(2,1)S(1)} %bitcast.5), custom_call_target="tpu_custom_call" | custom-call | tf_op jit(solution)/shard_map/place/pallas_call | solution.py:484

commit v2 on v1

--- a/solution.py
+++ b/solution.py
@@ -11,6 +11,7 @@
 EPS = 1e-05
 CHUNKS = 16
 LEAD = 4
+SIDE = 4
 TAIL = 2
 STATS_AT = 4
 HALF_AT = 9
@@ -30,24 +31,25 @@
     return out
 
 
-def mask_at(me, step, groups):
+def peer_mask(me, step, groups, early):
     quarter = groups // 4
-    inner = ((me // quarter + 1) // 2) % 2
-    turn = step // quarter
-    first = (3 - turn) // 3
-    second = (turn % 2) * (1 - turn // 2)
-    third = (turn // 2) * (1 - turn % 2)
-    far = first * (1 + inner) + 3 * second + third * (2 - inner)
-    return far * quarter + quarter - 1 - step % quarter
-
-
-def peer_mask(me, step, groups, early):
-    regular = groups - early
-    split = groups // 2 - early
-    is_early = step // regular
-    after = (1 + step // split) // 2
-    late = step - regular + split
-    return mask_at(me, is_early * late + (1 - is_early) * (step + early * after), groups)
+    half = quarter // 2
+    one, two, three = ((far + 1) * quarter - 1 for far in (1, 2, 3))
+    outer = ((one, quarter), (three, quarter - early), (two, quarter), (quarter - 1, quarter))
+    inner = (
+        (two, quarter), (quarter - 1, half), (three, quarter - early), (one, quarter), (half - 1, half)
+    )
+
+    def mask_in(runs):
+        out = 0
+        begin = 0
+        for first, length in (*runs, (3 * quarter + early - 1, early)):
+            out = jnp.where(step >= begin, first + begin - step, out)
+            begin += length
+        return out
+
+    middle = ((me // quarter + 1) // 2) % 2
+    return jnp.where(middle == 1, mask_in(inner), mask_in(outer))
 
 
 def ranked(offset, value, capacity):
@@ -87,7 +89,7 @@
     table, listed, index, raw, away, mine, others, weight, keys, normed, ready, gains, total,
     columns_stat, own_stat, peer_stat, means, scales,
     table_sem, index_sem, raw_sem, early_send, early_recv, weight_sem, gain_sem, gather_send, gather_recv,
-    last_send, last_recv, stat_send, stat_recv, key_send, key_recv,
+    last_send, last_recv, stat_send, stat_recv, key_send, key_recv, met,
 ):
     me = lax.axis_index("grp")
     part = lax.axis_index("tp")
@@ -110,6 +112,8 @@
 
     table_copy = pltpu.make_async_copy(table_ref, table, table_sem)
     table_copy.start()
+    line = me // SIDE
+    lines = groups // SIDE
     loads = min(LOADS, blocks)
     for i in range(loads):
         at = pl.ds(i * (blocks // loads), blocks // loads)
@@ -119,18 +123,21 @@
 
     barrier = pltpu.get_barrier_semaphore()
 
-    def greet(i, carry):
-        mask = groups - i
-        pl.semaphore_signal(
-            barrier, inc=1, device_id={"grp": flipped(me, mask, groups)}, device_id_type=MESH
-        )
-        return carry
-
-    lax.fori_loop(1, groups, greet, 0)
+    def greet(sem, device):
+        pl.semaphore_signal(sem, inc=1, device_id=device, device_id_type=MESH)
+
     for j in range(1, parts):
-        pl.semaphore_signal(
-            barrier, inc=1, device_id={"tp": (part + j) % parts}, device_id_type=MESH
-        )
+        greet(barrier, {"tp": (part + j) % parts})
+    for bit in range(2):
+        greet(barrier, {"grp": flipped(me, 1 << bit, SIDE)})
+
+    @pl.when(line > 0)
+    def _():
+        greet(barrier, {"grp": me - SIDE})
+
+    @pl.when(line < lines - 1)
+    def _():
+        greet(barrier, {"grp": me + SIDE})
 
     def weight_copy(j):
         origin = (part + j) % parts
@@ -230,16 +237,72 @@
 
     arrange(0)
     arrange(last)
-    pl.semaphore_wait(barrier, groups - 1 + parts - 1)
-    for j in range(1, parts):
-        gather_copy(0, j).start()
-    for i in range(per_chunk):
-        early_copy(i).start()
-    for c in range(1, last):
+    inner = (line > 0) & (line < lines - 1)
+    neighbours = 1 + inner.astype(jnp.int32)
+    pl.semaphore_wait(barrier, parts - 1 + 2 + neighbours)
+
+    def gather(c):
+        for j in range(1, parts):
+            gather_copy(c, j).start()
+
+    def send_early():
+        for i in range(per_chunk):
+            early_copy(i).start()
+
+    gather(0)
+    near = lines == 4 and per_chunk == 1
+    if near:
+
+        @pl.when(inner)
+        def _():
+            send_early()
+
+    arrange(1)
+    gather(1)
+
+    def from_below():
+        @pl.when(line > 1)
+        def _():
+            pl.semaphore_wait(met.at[0], 1)
+
+        @pl.when((line > 0) & (line < lines - 1))
+        def _():
+            greet(met.at[0], {"grp": me + SIDE})
+
+    def from_above():
+        @pl.when(line < lines - 2)
+        def _():
+            pl.semaphore_wait(met.at[1], 1)
+
+        @pl.when((line > 0) & (line < lines - 1))
+        def _():
+            greet(met.at[1], {"grp": me - SIDE})
+
+    @pl.when(line < lines // 2)
+    def _():
+        from_below()
+        from_above()
+
+    @pl.when(line >= lines // 2)
+    def _():
+        from_above()
+        from_below()
+
+    if near:
+
+        @pl.when(jnp.logical_not(inner))
+        def _():
+            send_early()
+
+    for bit in range(2):
+        greet(met.at[2 + bit], {"grp": flipped(me, 1 << bit, SIDE)})
+        pl.semaphore_wait(met.at[2 + bit], 1)
+    if not near:
+        send_early()
+    for c in range(2, last):
         arrange(c)
         if c < LEAD:
-            for j in range(1, parts):
-                gather_copy(c, j).start()
+            gather(c)
 
     offset = table[...] - me * blocks
     slot_ref[...] = ranked(offset, offset, capacity)
@@ -469,6 +532,7 @@
             dma((parts - 1,)),
             dma((groups,)),
             dma((groups,)),
+            pltpu.SemaphoreType.REGULAR((4,)),
         ],
         compiler_params=pltpu.CompilerParams(
             collective_id=0, has_side_effects=True, vmem_limit_bytes=48 * MIB

time: 104 us -> 101 us (0.971)
  Pallas kernels: 103 us -> 101 us
    pallas_call x1, Pallas kernels: 100 us -> 98.5 us  [on_device(): pl.pallas_call(functools.partial(main_kernel, groups, parts), out_shape=[...]
where the time goes in v2:
time: 101 us
  Pallas kernels  101 us (100%)
    pallas_call x1, Pallas kernels, on_device(): pl.pallas_call(functools.partial(main_kernel, groups, parts), out_shape=[...  98.5 us
    pallas_call x1, Pallas kernels, on_device(): pl.pallas_call(functools.partial(place_kernel, groups), out_shape=jax.Sha...  2.64 us

profile of v2, /device:TPU:0, one launch (start us, length us, event | category | flops | bytes accessed | tf_op | source)
XLA Modules:
  0.0 101.1 jit_solution(16392518384807165843)
XLA Ops:
  0.0 98.5 %exchange.1 = (bf16[1024,2048]{1,0:T(8,128)(2,1)S(1)}, s32[16,128]{1,0:T(8,128)S(1)}) custom-call(s32[16,128]{1,0:T(8,128)} %bitcast.8, bf16[128,8,2048]{2,1,0:T(8,128)(2,1)} %bitcast.6, f32[1,4096]{1,0:T(1,128)} %bitcast.7, bf16[4096,2048]{1,0:T(8,128)(2,1)} %weight_ref.1), custom_call_target="tpu_custom_call" | custom-call | tf_op jit(solution)/shard_map/exchange/pallas_call | solution.py:493
  98.5 2.6 %place.1 = bf16[128,8,2048]{2,1,0:T(8,128)(2,1)} custom-call(s32[16,128]{1,0:T(8,128)S(1)} %get-tuple-element.7.slot_ref, bf16[128,8,2048]{2,1,0:T(8,128)(2,1)S(1)} %bitcast.5), custom_call_target="tpu_custom_call" | custom-call | tf_op jit(solution)/shard_map/place/pallas_call | solution.py:548

commit v3 on v2

--- a/solution.py
+++ b/solution.py
@@ -73,14 +73,12 @@
     me = lax.axis_index("grp")
     blocks = in_ref.shape[0]
     capacity = blocks // groups
-
-    def move(mask, carry):
+    for mask in range(groups):
+        slots = slot_ref[pl.ds(me ^ mask, 1), :]
         for r in range(capacity):
-            slot = slot_ref[me ^ mask, r]
-            pltpu.make_async_copy(in_ref.at[mask * capacity + r], out_ref.at[slot], sem).start()
-        return carry
-
-    lax.fori_loop(0, groups, move, 0)
+            pltpu.make_async_copy(
+                in_ref.at[mask * capacity + r], out_ref.at[slots[0, r]], sem
+            ).start()
     pltpu.make_async_copy(in_ref, out_ref, sem).wait()
 
 
@@ -195,6 +193,16 @@
             device_id_type=MESH,
         )
 
+    def key_wait(step, mask):
+        return pltpu.make_async_remote_copy(
+            src_ref=keys.at[pl.ds(step * piece, piece)],
+            dst_ref=out_ref.at[pl.ds(mask * piece, piece)],
+            send_sem=key_send.at[step],
+            recv_sem=key_recv.at[mask],
+            device_id={"grp": flipped(me, 1, SIDE)},
+            device_id_type=MESH,
+        )
+
     def early_copy(i):
         mask = peer_mask(me, regular + i, groups, per_chunk)
         return pltpu.make_async_remote_copy(
@@ -230,13 +238,13 @@
     listed[...] = ranked(own - peer * blocks, lane, capacity)
     index_copy = pltpu.make_async_copy(listed, index, index_sem)
     index_copy.start()
-    index_copy.wait()
     pltpu.make_async_copy(rows_ref, raw, raw_sem).wait()
     for j in range(parts):
         weight_copy(j).start()
 
-    arrange(0)
-    arrange(last)
+    for i in range(chunk_blocks):
+        at = listed[pl.ds(i // capacity, 1), pl.ds(i % capacity, 1)][0, 0]
+        mine[i] = raw[jnp.minimum(jnp.maximum(at, 0), blocks - 1)]
     inner = (line > 0) & (line < lines - 1)
     neighbours = 1 + inner.astype(jnp.int32)
     pl.semaphore_wait(barrier, parts - 1 + 2 + neighbours)
@@ -250,6 +258,8 @@
             early_copy(i).start()
 
     gather(0)
+    index_copy.wait()
+    arrange(last)
     near = lines == 4 and per_chunk == 1
     if near:
 
@@ -424,6 +434,18 @@
 
     lax.fori_loop(0, body, one_chunk, 0)
 
+    for i in range(per_chunk):
+        early_copy(i).wait_send()
+    for j in range(1, parts):
+        stat_copy(j).wait_send()
+
+    def sent(c, carry):
+        for j in range(1, parts):
+            gather_copy(c, j).wait_send()
+        return carry
+
+    lax.fori_loop(0, body, sent, 0)
+
     def last_slice(s, j):
         first = s * slice_width
         last_copy(j, s).wait_recv()
@@ -448,30 +470,18 @@
             mask = peer_mask(me, step, groups, per_chunk)
             out_ref[pl.ds(pl.multiple_of(mask * piece, piece), piece), :] = rows
 
-    for i in range(per_chunk):
-        early_copy(i).wait_send()
-    for j in range(1, parts):
-        stat_copy(j).wait_send()
-
-    def sent(c, carry):
-        for j in range(1, parts):
-            gather_copy(c, j).wait_send()
-        return carry
-
-    lax.fori_loop(0, body, sent, 0)
-
     def last_sent(s, carry):
         for j in range(1, parts):
             last_copy(j, s).wait_send()
         return carry
 
     lax.fori_loop(0, slices, last_sent, 0)
-
-    def finish(step, carry):
-        key_copy(step).wait()
-        return carry
-
-    lax.fori_loop(0, regular - 1, finish, 0)
+    early = [3 * (groups // 4) + i for i in range(per_chunk)]
+    for step in range(regular - 1):
+        key_wait(step, 0).wait_send()
+    for mask in range(1, groups):
+        if mask not in early:
+            key_wait(0, mask).wait_recv()
 
 
 def on_device(groups, parts, memory_rows, norm_gain, key_weight, owner_table):
@@ -484,7 +494,6 @@
     any_space = pl.BlockSpec(memory_space=pl.ANY)
     in_hbm = pl.BlockSpec(memory_space=pltpu.HBM)
     in_vmem = pl.BlockSpec(memory_space=pltpu.VMEM)
-    in_smem = pl.BlockSpec(memory_space=pltpu.SMEM)
 
     def kept(x):
         return pltpu.with_memory_space_constraint(x, pltpu.HBM)
@@ -548,9 +557,9 @@
     placed = pl.pallas_call(
         functools.partial(place_kernel, groups),
         out_shape=jax.ShapeDtypeStruct((blocks, BLK_ROWS, columns), jnp.bfloat16),
-        in_specs=[in_smem, in_vmem],
+        in_specs=[in_vmem, in_vmem],
         out_specs=any_space,
-        scratch_shapes=[pltpu.SemaphoreType.DMA],
+        scratch_shapes=[dma],
         compiler_params=pltpu.CompilerParams(vmem_limit_bytes=16 * MIB),
         name="place",
     )(slots, incoming.reshape(blocks, BLK_ROWS, columns))

time: 101 us -> 99.6 us (0.986)
  Pallas kernels: 101 us -> 99.5 us
    pallas_call x1, Pallas kernels: 98.5 us -> 97.4 us  [on_device(): pl.pallas_call(functools.partial(main_kernel, groups, parts), out_shape=[...]
where the time goes in v3:
time: 99.6 us; the launch traced here: 99.5 us
  Pallas kernels  99.5 us (100%)
    pallas_call x1, Pallas kernels, on_device(): pl.pallas_call(functools.partial(main_kernel, groups, parts), out_shape=[...  97.4 us
    pallas_call x1, Pallas kernels, on_device(): pl.pallas_call(functools.partial(place_kernel, groups), out_shape=jax.Sha...  2.07 us

profile of v3, /device:TPU:0, one launch (start us, length us, event | category | flops | bytes accessed | tf_op | source)
XLA Modules:
  0.0 99.5 jit_solution(2272235681979798605)
XLA Ops:
  0.0 97.4 %exchange.1 = (bf16[1024,2048]{1,0:T(8,128)(2,1)S(1)}, s32[16,128]{1,0:T(8,128)S(1)}) custom-call(s32[16,128]{1,0:T(8,128)} %bitcast.8, bf16[128,8,2048]{2,1,0:T(8,128)(2,1)} %bitcast.6, f32[1,4096]{1,0:T(1,128)} %bitcast.7, bf16[4096,2048]{1,0:T(8,128)(2,1)} %weight_ref.1), custom_call_target="tpu_custom_call" | custom-call | tf_op jit(solution)/shard_map/exchange/pallas_call | solution.py:502
  97.4 2.1 %place.1 = bf16[128,8,2048]{2,1,0:T(8,128)(2,1)} custom-call(s32[16,128]{1,0:T(8,128)S(1)} %get-tuple-element.7.slot_ref, bf16[128,8,2048]{2,1,0:T(8,128)(2,1)S(1)} %bitcast.5), custom_call_target="tpu_custom_call" | custom-call | tf_op jit(solution)/shard_map/place/pallas_call | solution.py:557

commit v4 on v3

--- a/solution.py
+++ b/solution.py
@@ -15,7 +15,7 @@
 TAIL = 2
 STATS_AT = 4
 HALF_AT = 9
-SLICE = 256
+SLICE = 128
 LANES = 128
 LOADS = 8
 MIB = 1024 * 1024

time: 99.6 us -> 99.8 us (level)
  no operation moved by 1% of the time
where the time goes in v4:
time: 99.8 us; the launch traced here: 99.7 us
  Pallas kernels  99.7 us (100%)
    pallas_call x1, Pallas kernels, on_device(): pl.pallas_call(functools.partial(main_kernel, groups, parts), out_shape=[...  97.6 us
    pallas_call x1, Pallas kernels, on_device(): pl.pallas_call(functools.partial(place_kernel, groups), out_shape=jax.Sha...  2.07 us

profile of v4, /device:TPU:0, one launch (start us, length us, event | category | flops | bytes accessed | tf_op | source)
XLA Modules:
  0.0 99.7 jit_solution(6554214223443674379)
XLA Ops:
  0.0 97.6 %exchange.1 = (bf16[1024,2048]{1,0:T(8,128)(2,1)S(1)}, s32[16,128]{1,0:T(8,128)S(1)}) custom-call(s32[16,128]{1,0:T(8,128)} %bitcast.8, bf16[128,8,2048]{2,1,0:T(8,128)(2,1)} %bitcast.6, f32[1,4096]{1,0:T(1,128)} %bitcast.7, bf16[4096,2048]{1,0:T(8,128)(2,1)} %weight_ref.1), custom_call_target="tpu_custom_call" | custom-call | tf_op jit(solution)/shard_map/exchange/pallas_call | solution.py:502
  97.6 2.1 %place.1 = bf16[128,8,2048]{2,1,0:T(8,128)(2,1)} custom-call(s32[16,128]{1,0:T(8,128)S(1)} %get-tuple-element.7.slot_ref, bf16[128,8,2048]{2,1,0:T(8,128)(2,1)S(1)} %bitcast.5), custom_call_target="tpu_custom_call" | custom-call | tf_op jit(solution)/shard_map/place/pallas_call | solution.py:557
